TPU v7x, 32 devices: a whole 2x2x4 slice. The times are simulated.
32 devices in a mesh: scen: 2 (over y), row: 4 (over z), col: 2 (over x), layer: 2 (over core).
Axes of the slice: x: 2, y: 2, z: 4, core: 2. Of those that a mesh axis runs over, the one named last changes fastest.
Arguments:
- current: float32 [2, 1024, 2048], P('layer', ('scen', 'row'), 'col'), parts along dimension 1, may hold values from 0.5 to 10
- node_class: int32 [2, 1024, 2048], P('layer', ('scen', 'row'), 'col'), parts along dimension 1, may hold values from 0 to 7
- class_conductance: float32 [2, 8], P('layer'), may hold values from 0.5 to 4
- pad_mask: int32 [2, 1024, 2048], P('layer', ('scen', 'row'), 'col'), parts along dimension 1, may hold values 0 or 1
- via_mask: int32 [1024, 2048], P(('scen', 'row'), 'col'), parts along dimension 0, may hold values 0 or 1
Outputs:
- drop: float32 [2, 1024, 2048], P('layer', ('scen', 'row'), 'col'), parts along dimension 1
- residual: float32 [2, 1024, 2048], P('layer', ('scen', 'row'), 'col'), parts along dimension 1
- worst: float32 [2, 1024, 2048], P('layer', ('scen', 'row'), 'col'), parts along dimension 1
There are 2 independent parts, one for each index of `scen`. A program takes and returns all parts, laid end to end along the dimension named above; an argument that names none is the same for every part. Nothing has to cross between parts.
All inputs are finite; a program needn't handle non-finite values. No bound on the sum of `pad_mask` or of `via_mask` on one device may be relied on, other than what follows from the above.
Results may differ from a plain program's by a relative error of at most 0.0003.
Values sent between devices are 32-bit elements; how exact they have to be, the bound alone decides.
A program may use at most 64 MiB of HBM per device.

v0:
```python
import jax
import jax.numpy as jnp
from jax import lax
from jax.sharding import PartitionSpec as P

ITERS = 2


via_conductance = 2.0
pad_conductance = 4.0
leakage = 0.05


def extended(cells, sides, width):
    for axis, dim in sides:
        count = lax.axis_size(axis)
        ends = count - 1
        head = lax.slice_in_dim(cells, 0, width, axis=dim)
        tail = lax.slice_in_dim(cells, cells.shape[dim] - width, cells.shape[dim], axis=dim)
        cells = jnp.concatenate(
            [
                lax.ppermute(tail, axis, [(i, (i + 1) % count) for i in range(ends)]),
                cells,
                lax.ppermute(head, axis, [((i + 1) % count, i) for i in range(ends)]),
            ],
            axis=dim,
        )
    return cells


def from_partner(value, axis, stride):
    return lax.ppermute(value, axis, [(i, i ^ 1 << stride) for i in range(lax.axis_size(axis))])


def lookup(node_class, class_conductance):
    cond = jnp.zeros(node_class.shape, jnp.float32)
    for klass in range(class_conductance.shape[1]):
        cond = cond + jnp.where(
            node_class == klass, class_conductance[:, klass][:, None, None], jnp.float32(0.0)
        )
    return cond


def edge_terms(cond):
    padded = extended(cond, (("row", 1), ("col", 2)), 1)
    beside_all = (
        padded[:, :-2, 1:-1],
        padded[:, 2:, 1:-1],
        padded[:, 1:-1, :-2],
        padded[:, 1:-1, 2:],
    )
    return tuple(
        (jnp.where(other > 0.0, 0.5 * (cond + other), jnp.float32(0.0)) for other in beside_all)
    )


def apply_grid(values, edges, diagonal, coupling):
    padded = extended(values, (("row", 1), ("col", 2)), 1)
    partner = from_partner(values, "layer", 0)
    beside = edges[0] * padded[:, :-2, 1:-1] + edges[1] * padded[:, 2:, 1:-1]
    beside = beside + edges[2] * padded[:, 1:-1, :-2] + edges[3] * padded[:, 1:-1, 2:]
    return diagonal * values - beside - coupling * partner


def local(current, node_class, class_conductance, pad_mask, via_mask):
    cond = lookup(node_class, class_conductance)
    edges = edge_terms(cond)
    coupling = via_conductance * via_mask.astype(jnp.float32)
    diagonal = (
        edges[0]
        + edges[1]
        + edges[2]
        + edges[3]
        + coupling
        + pad_conductance * pad_mask.astype(jnp.float32)
        + leakage
    )
    drop_field = jnp.zeros_like(current)
    resid = current
    worst_field = drop_field

    def inner_pair(resid_now):
        precond_now = resid_now / diagonal
        image_now = apply_grid(precond_now, edges, diagonal, coupling)
        energy_part, curve_part = lax.psum(
            (jnp.sum(resid_now * precond_now), jnp.sum(precond_now * image_now)),
            ("row", "col", "layer"),
        )
        return (precond_now, image_now, energy_part, curve_part)

    precond, image, energy_now, curve_now = inner_pair(resid)
    step_size = energy_now / curve_now
    direction, along = (precond, image)
    for iteration in range(ITERS):
        drop_field = drop_field + step_size * direction
        resid = resid - step_size * along
        worst_field = drop_field if iteration == 0 else jnp.maximum(worst_field, drop_field)
        if iteration + 1 < ITERS:
            precond, image, energy_next, curve_now = inner_pair(resid)
            ratio = energy_next / energy_now
            step_size = energy_next / (curve_now - ratio * energy_next / step_size)
            direction = precond + ratio * direction
            along = image + ratio * along
            energy_now = energy_next
    return (drop_field, resid, worst_field)


def solution(mesh):
    in_specs = (
        P("layer", ("scen", "row"), "col"),
        P("layer", ("scen", "row"), "col"),
        P("layer", None),
        P("layer", ("scen", "row"), "col"),
        P(("scen", "row"), "col"),
    )
    out_specs = (
        P("layer", ("scen", "row"), "col"),
        P("layer", ("scen", "row"), "col"),
        P("layer", ("scen", "row"), "col"),
    )
    return jax.shard_map(local, mesh=mesh, in_specs=in_specs, out_specs=out_specs, check_vma=False)
```

profile of v0, /device:TPU:0, one launch (start us, length us, event | category | flops | bytes accessed | tf_op | source)
XLA Modules:
  0.0 133.7 jit_solution(16382097239738526229)
XLA Ops:
  0.6 1.6 %fusion.44 = (f32[1,1]{1,0:T(1,128)}, f32[1,1]{1,0:T(1,128)}, f32[1,1]{1,0:T(1,128)}, f32[1,1]{1,0:T(1,128)}, f32[1,1]{1,0:T(1,128)}, /*index=5*/f32[1,1]{1,0:T(1,128)}, f32[1,1]{1,0:T(1,128)}, f32[1,1]{1,0:T(1,128)}) fusion(f32[1,8]{1,0:T(1,128)} %param.7), kind=kLoop, calls=%fused_computation.87 | loop fusion | bytes 64 | tf_op jit(solution)/shard_map/slice | solution.py:39
  2.2 6.5 %select_add_fusion = f32[1,128,1024]{2,1,0:T(8,128)S(1)} fusion(s32[1,128,1024]{2,1,0:T(8,128)} %param.6, f32[]{:T(128)} %bitcast.7, f32[]{:T(128)} %bitcast.6, f32[]{:T(128)} %bitcast.5, f32[]{:T(128)} %bitcast.4, f32[]{:T(128)} %bitcast.3, f32[]{:T(128)} %bitcast.2, f32[]{:T(128)} %bitcast.1, f32[]{:T(128)} %bitcast), kind=kLoop, calls=%fused_computation.71 | loop fusion | flops 3014656 | bytes 1048608 | tf_op jit(solution)/shard_map/add | solution.py:38
  8.7 5.1 %collective-permute-start = (f32[1,1,1024]{2,1,0:T(1,128)S(1)}, f32[1,1,1024]{2,1,0:T(1,128)S(1)}, u32[]{:S(2)}, u32[]{:S(2)}) collective-permute-start(f32[1,1,1024]{2,1,0:T(1,128)S(1)} %get-tuple-element.27), channel_id=1, source_target_pairs={{0,4},{4,8},{8,12},{1,5},{5,9},{9,13},{2,6},{6,10},{10,14},{3,7},{... | collective-permute-start | bytes 12296 | tf_op jit(solution)/shard_map/ppermute | solution.py:22
  13.8 1.3 collective-permute-start.1
  15.1 4.2 %collective-permute-done.1 = f32[1,1,1024]{2,1,0:T(1,128)S(1)} collective-permute-done((f32[1,1,1024]{2,1,0:T(1,128)S(1)}, f32[1,1,1024]{2,1,0:T(1,128)S(1)}, u32[]{:S(2)}, u32[]{:S(2)}) %collective-permute-start.1) | collective-permute-done | bytes 4128 | tf_op jit(solution)/shard_map/ppermute | solution.py:24
  19.4 3.4 %collective-permute-start.2 = (f32[1,130,1]{2,1,0:T(8,128)S(1)}, f32[1,130,1]{2,1,0:T(8,128)S(1)}, u32[]{:S(2)}, u32[]{:S(2)}) collective-permute-start(f32[1,130,1]{2,1,0:T(8,128)S(1)} %get-tuple-element.21), channel_id=1, source_target_pairs={{0,2},{1,3},{4,6},{5,7},{8,10},{9,11},{12,14},{13,15},{16,18},{17,... | collective-permute-start | bytes 1568 | tf_op jit(solution)/shard_map/ppermute | solution.py:22
  22.8 1.3 collective-permute-start.3
  24.7 4.3 %collective-permute-done.3 = f32[1,130,1]{2,1,0:T(8,128)S(1)} collective-permute-done((f32[1,130,1]{2,1,0:T(8,128)S(1)}, f32[1,130,1]{2,1,0:T(8,128)S(1)}, u32[]{:S(2)}, u32[]{:S(2)}) %collective-permute-start.3) | collective-permute-done | bytes 552 | tf_op jit(solution)/shard_map/ppermute | solution.py:24
  29.8 3.5 %collective-permute-start.4 = (f32[1,1,1024]{2,1,0:T(1,128)S(1)}, f32[1,1,1024]{2,1,0:T(1,128)S(1)}, u32[]{:S(2)}, u32[]{:S(2)}) collective-permute-start(f32[1,1,1024]{2,1,0:T(1,128)S(1)} %get-tuple-element.25), channel_id=1, source_target_pairs={{0,4},{4,8},{8,12},{1,5},{5,9},{9,13},{2,6},{6,10},{10,14},{3,7},{... | collective-permute-start | bytes 12296 | tf_op jit(solution)/shard_map/ppermute | solution.py:22
  33.3 1.3 collective-permute-start.5
  34.6 4.2 %collective-permute-done.5 = f32[1,1,1024]{2,1,0:T(1,128)S(1)} collective-permute-done((f32[1,1,1024]{2,1,0:T(1,128)S(1)}, f32[1,1,1024]{2,1,0:T(1,128)S(1)}, u32[]{:S(2)}, u32[]{:S(2)}) %collective-permute-start.5) | collective-permute-done | bytes 4128 | tf_op jit(solution)/shard_map/ppermute | solution.py:24
  38.9 1.6 %collective-permute-start.6 = (f32[1,130,1]{2,1,0:T(8,128)S(1)}, f32[1,130,1]{2,1,0:T(8,128)S(1)}, u32[]{:S(2)}, u32[]{:S(2)}) collective-permute-start(f32[1,130,1]{2,1,0:T(8,128)S(1)} %get-tuple-element.19), channel_id=1, source_target_pairs={{0,2},{1,3},{4,6},{5,7},{8,10},{9,11},{12,14},{13,15},{16,18},{17,... | collective-permute-start | bytes 1568 | tf_op jit(solution)/shard_map/ppermute | solution.py:22
  40.5 1.3 collective-permute-start.7
  42.4 4.3 %collective-permute-done.7 = f32[1,130,1]{2,1,0:T(8,128)S(1)} collective-permute-done((f32[1,130,1]{2,1,0:T(8,128)S(1)}, f32[1,130,1]{2,1,0:T(8,128)S(1)}, u32[]{:S(2)}, u32[]{:S(2)}) %collective-permute-start.7) | collective-permute-done | bytes 552 | tf_op jit(solution)/shard_map/ppermute | solution.py:24
  46.7 1.5 %multiply_reduce_fusion.2 = (f32[]{:T(128)}, f32[]{:T(128)}, f32[1,128,1024]{2,1,0:T(8,128)S(1)}) fusion(f32[1,128,1024]{2,1,0:T(8,128)S(1)} %get-tuple-element.15, f32[1,128,1024]{2,1,0:T(8,128)S(1)} %copy-done, f32[1,128,1024]{2,1,0:T(8,128)S(1)} %collective-permute-done.8, s32[128,1024]{1,0:T(8,128)S(1)} %copy-done.1, ...), kind=kLoop, calls=%fused_computation.68 | loop fusion | flops 6422526 | bytes 3688488 | tf_op jit(solution)/shard_map/reduce_sum | solution.py:86
  48.1 30.1 %all-reduce.1 = (f32[]{:T(128)}, f32[]{:T(128)}) all-reduce(f32[]{:T(128)} %get-tuple-element.6, f32[]{:T(128)} %get-tuple-element.5), channel_id=1, replica_groups=mesh['scen'=2,'row'=4,'col'=2,'layer'=2] {'row','col','layer'}, use_global_device_ids=true, to_apply=%region_1.2 | all-reduce | flops 2 | bytes 16 | tf_op jit(solution)/shard_map/psum | solution.py:85
  79.8 1.4 %collective-permute-start.9 = (f32[1,1,1024]{2,1,0:T(1,128)S(1)}, f32[1,1,1024]{2,1,0:T(1,128)S(1)}, u32[]{:S(2)}, u32[]{:S(2)}) collective-permute-start(f32[1,1,1024]{2,1,0:T(1,128)S(1)} %get-tuple-element.23), channel_id=1, source_target_pairs={{0,4},{4,8},{8,12},{1,5},{5,9},{9,13},{2,6},{6,10},{10,14},{3,7},{... | collective-permute-start | bytes 12296 | tf_op jit(solution)/shard_map/ppermute | solution.py:22
  81.3 1.3 collective-permute-start.10
  82.6 4.2 %collective-permute-done.10 = f32[1,1,1024]{2,1,0:T(1,128)S(1)} collective-permute-done((f32[1,1,1024]{2,1,0:T(1,128)S(1)}, f32[1,1,1024]{2,1,0:T(1,128)S(1)}, u32[]{:S(2)}, u32[]{:S(2)}) %collective-permute-start.10) | collective-permute-done | bytes 4128 | tf_op jit(solution)/shard_map/ppermute | solution.py:24
  86.9 1.3 collective-permute-start.11
  90.1 4.3 %collective-permute-done.12 = f32[1,130,1]{2,1,0:T(8,128)S(1)} collective-permute-done((f32[1,130,1]{2,1,0:T(8,128)S(1)}, f32[1,130,1]{2,1,0:T(8,128)S(1)}, u32[]{:S(2)}, u32[]{:S(2)}) %collective-permute-start.12) | collective-permute-done | bytes 552 | tf_op jit(solution)/shard_map/ppermute | solution.py:24
  94.4 2.3 %multiply_reduce_fusion = (f32[]{:T(128)}, f32[]{:T(128)}, f32[1,128,1024]{2,1,0:T(8,128)}) fusion(f32[1,128,1024]{2,1,0:T(8,128)S(1)} %fusion.36, f32[1,128,1024]{2,1,0:T(8,128)S(1)} %copy-done, f32[1,128,1024]{2,1,0:T(8,128)S(1)} %get-tuple-element.14, f32[]{:T(128)S(6)} %div.19, f32[1,128,1024]{2,1,0:T(8,128)S(1)} %collective-permute-done.13, ...), kind=kLoop, calls=%fused_computation.65 | loop fusion | flops 6684670 | bytes 4212780 | tf_op jit(solution)/shard_map/reduce_sum | solution.py:86
  96.7 30.2 %all-reduce = (f32[]{:T(128)}, f32[]{:T(128)}) all-reduce(f32[]{:T(128)} %get-tuple-element.4, f32[]{:T(128)} %get-tuple-element.3), channel_id=1, replica_groups=mesh['scen'=2,'row'=4,'col'=2,'layer'=2] {'row','col','layer'}, use_global_device_ids=true, to_apply=%region_5.6 | all-reduce | flops 2 | bytes 16 | tf_op jit(solution)/shard_map/psum | solution.py:85
  131.4 2.3 %multiply_maximum_fusion = (f32[1,128,1024]{2,1,0:T(8,128)}, f32[1,128,1024]{2,1,0:T(8,128)}, f32[1,128,1024]{2,1,0:T(8,128)}) fusion(f32[1,128,1024]{2,1,0:T(8,128)S(1)} %get-tuple-element.15, f32[]{:T(128)S(6)} %div.19, f32[1,128,1024]{2,1,0:T(8,128)S(1)} %fusion.36, f32[]{:T(128)S(6)} %div.21, f32[]{:T(128)S(6)} %div.23, ...), kind=kLoop, calls=%fused_computation.72 | loop fusion | flops 1572864 | bytes 4194316 | tf_op jit(solution)/shard_map/max | solution.py:97
  (27 shorter events, 4.4 us)
Async XLA Ops:
  2.2 26.8 %copy-start.1 = (s32[128,1024]{1,0:T(8,128)S(1)}, s32[128,1024]{1,0:T(8,128)}, u32[]{:S(2)}) copy-start(s32[128,1024]{1,0:T(8,128)} %param.9) | copy-start | bytes 1572868
  2.2 26.8 %copy-start.3 = (s32[1,128,1024]{2,1,0:T(8,128)S(1)}, s32[1,128,1024]{2,1,0:T(8,128)}, u32[]{:S(2)}) copy-start(s32[1,128,1024]{2,1,0:T(8,128)} %param.8) | copy-start | bytes 1572868
  8.7 20.3 %copy-start = (f32[1,128,1024]{2,1,0:T(8,128)S(1)}, f32[1,128,1024]{2,1,0:T(8,128)}, u32[]{:S(2)}) copy-start(f32[1,128,1024]{2,1,0:T(8,128)} %param.5) | copy-start | bytes 1572868
  8.7 6.4 %collective-permute-start = (f32[1,1,1024]{2,1,0:T(1,128)S(1)}, f32[1,1,1024]{2,1,0:T(1,128)S(1)}, u32[]{:S(2)}, u32[]{:S(2)}) collective-permute-start(f32[1,1,1024]{2,1,0:T(1,128)S(1)} %get-tuple-element.27), channel_id=1, source_target_pairs={{0,4},{4,8},{8,12},{1,5},{5,9},{9,13},{2,6},{6,10},{10,14},{3,7},{... | collective-permute-start | bytes 12296 | tf_op jit(solution)/shard_map/ppermute | solution.py:22
  13.8 5.5 %collective-permute-start.1 = (f32[1,1,1024]{2,1,0:T(1,128)S(1)}, f32[1,1,1024]{2,1,0:T(1,128)S(1)}, u32[]{:S(2)}, u32[]{:S(2)}) collective-permute-start(f32[1,1,1024]{2,1,0:T(1,128)S(1)} %get-tuple-element.28), channel_id=1, source_target_pairs={{4,0},{8,4},{12,8},{5,1},{9,5},{13,9},{6,2},{10,6},{14,10},{7,3},{... | collective-permute-start | bytes 12296 | tf_op jit(solution)/shard_map/ppermute | solution.py:24
  19.4 5.3 %collective-permute-start.2 = (f32[1,130,1]{2,1,0:T(8,128)S(1)}, f32[1,130,1]{2,1,0:T(8,128)S(1)}, u32[]{:S(2)}, u32[]{:S(2)}) collective-permute-start(f32[1,130,1]{2,1,0:T(8,128)S(1)} %get-tuple-element.21), channel_id=1, source_target_pairs={{0,2},{1,3},{4,6},{5,7},{8,10},{9,11},{12,14},{13,15},{16,18},{17,... | collective-permute-start | bytes 1568 | tf_op jit(solution)/shard_map/ppermute | solution.py:22
  22.8 6.2 %collective-permute-start.3 = (f32[1,130,1]{2,1,0:T(8,128)S(1)}, f32[1,130,1]{2,1,0:T(8,128)S(1)}, u32[]{:S(2)}, u32[]{:S(2)}) collective-permute-start(f32[1,130,1]{2,1,0:T(8,128)S(1)} %get-tuple-element.22), channel_id=1, source_target_pairs={{2,0},{3,1},{6,4},{7,5},{10,8},{11,9},{14,12},{15,13},{18,16},{19,... | collective-permute-start | bytes 1568 | tf_op jit(solution)/shard_map/ppermute | solution.py:24
  29.7 17.0 %collective-permute-start.8 = (f32[1,128,1024]{2,1,0:T(8,128)S(1)}, f32[1,128,1024]{2,1,0:T(8,128)S(1)}, u32[]{:S(2)}, u32[]{:S(2)}) collective-permute-start(f32[1,128,1024]{2,1,0:T(8,128)S(1)} %get-tuple-element.15), channel_id=1, source_target_pairs={{0,1},{1,0},{2,3},{3,2},{4,5},{5,4},{6,7},{7,6},{8,9},{9,8},{10,11... | collective-permute-start | bytes 1572872 | tf_op jit(solution)/shard_map/ppermute | solution.py:32
  29.8 4.8 %collective-permute-start.4 = (f32[1,1,1024]{2,1,0:T(1,128)S(1)}, f32[1,1,1024]{2,1,0:T(1,128)S(1)}, u32[]{:S(2)}, u32[]{:S(2)}) collective-permute-start(f32[1,1,1024]{2,1,0:T(1,128)S(1)} %get-tuple-element.25), channel_id=1, source_target_pairs={{0,4},{4,8},{8,12},{1,5},{5,9},{9,13},{2,6},{6,10},{10,14},{3,7},{... | collective-permute-start | bytes 12296 | tf_op jit(solution)/shard_map/ppermute | solution.py:22
  33.3 5.5 %collective-permute-start.5 = (f32[1,1,1024]{2,1,0:T(1,128)S(1)}, f32[1,1,1024]{2,1,0:T(1,128)S(1)}, u32[]{:S(2)}, u32[]{:S(2)}) collective-permute-start(f32[1,1,1024]{2,1,0:T(1,128)S(1)} %get-tuple-element.26), channel_id=1, source_target_pairs={{4,0},{8,4},{12,8},{5,1},{9,5},{13,9},{6,2},{10,6},{14,10},{7,3},{... | collective-permute-start | bytes 12296 | tf_op jit(solution)/shard_map/ppermute | solution.py:24
  38.9 3.5 %collective-permute-start.6 = (f32[1,130,1]{2,1,0:T(8,128)S(1)}, f32[1,130,1]{2,1,0:T(8,128)S(1)}, u32[]{:S(2)}, u32[]{:S(2)}) collective-permute-start(f32[1,130,1]{2,1,0:T(8,128)S(1)} %get-tuple-element.19), channel_id=1, source_target_pairs={{0,2},{1,3},{4,6},{5,7},{8,10},{9,11},{12,14},{13,15},{16,18},{17,... | collective-permute-start | bytes 1568 | tf_op jit(solution)/shard_map/ppermute | solution.py:22
  40.5 6.2 %collective-permute-start.7 = (f32[1,130,1]{2,1,0:T(8,128)S(1)}, f32[1,130,1]{2,1,0:T(8,128)S(1)}, u32[]{:S(2)}, u32[]{:S(2)}) collective-permute-start(f32[1,130,1]{2,1,0:T(8,128)S(1)} %get-tuple-element.20), channel_id=1, source_target_pairs={{2,0},{3,1},{6,4},{7,5},{10,8},{11,9},{14,12},{15,13},{18,16},{19,... | collective-permute-start | bytes 1568 | tf_op jit(solution)/shard_map/ppermute | solution.py:24
  79.7 14.6 %copy-start.2 = (s32[128,1024]{1,0:T(8,128)S(1)}, s32[128,1024]{1,0:T(8,128)}, u32[]{:S(2)}) copy-start(s32[128,1024]{1,0:T(8,128)} %param.9) | copy-start | bytes 1572868
  79.7 14.6 %collective-permute-start.13 = (f32[1,128,1024]{2,1,0:T(8,128)S(1)}, f32[1,128,1024]{2,1,0:T(8,128)S(1)}, u32[]{:S(2)}, u32[]{:S(2)}) collective-permute-start(f32[1,128,1024]{2,1,0:T(8,128)S(1)} %fusion.36), channel_id=1, source_target_pairs={{0,1},{1,0},{2,3},{3,2},{4,5},{5,4},{6,7},{7,6},{8,9},{9,8},{10,11... | collective-permute-start | bytes 1572872 | tf_op jit(solution)/shard_map/ppermute | solution.py:32
  79.8 2.7 %collective-permute-start.9 = (f32[1,1,1024]{2,1,0:T(1,128)S(1)}, f32[1,1,1024]{2,1,0:T(1,128)S(1)}, u32[]{:S(2)}, u32[]{:S(2)}) collective-permute-start(f32[1,1,1024]{2,1,0:T(1,128)S(1)} %get-tuple-element.23), channel_id=1, source_target_pairs={{0,4},{4,8},{8,12},{1,5},{5,9},{9,13},{2,6},{6,10},{10,14},{3,7},{... | collective-permute-start | bytes 12296 | tf_op jit(solution)/shard_map/ppermute | solution.py:22
  81.3 5.5 %collective-permute-start.10 = (f32[1,1,1024]{2,1,0:T(1,128)S(1)}, f32[1,1,1024]{2,1,0:T(1,128)S(1)}, u32[]{:S(2)}, u32[]{:S(2)}) collective-permute-start(f32[1,1,1024]{2,1,0:T(1,128)S(1)} %get-tuple-element.24), channel_id=1, source_target_pairs={{4,0},{8,4},{12,8},{5,1},{9,5},{13,9},{6,2},{10,6},{14,10},{7,3},{... | collective-permute-start | bytes 12296 | tf_op jit(solution)/shard_map/ppermute | solution.py:24
  86.9 3.2 %collective-permute-start.11 = (f32[1,130,1]{2,1,0:T(8,128)S(1)}, f32[1,130,1]{2,1,0:T(8,128)S(1)}, u32[]{:S(2)}, u32[]{:S(2)}) collective-permute-start(f32[1,130,1]{2,1,0:T(8,128)S(1)} %get-tuple-element.17), channel_id=1, source_target_pairs={{0,2},{1,3},{4,6},{5,7},{8,10},{9,11},{12,14},{13,15},{16,18},{17,... | collective-permute-start | bytes 1568 | tf_op jit(solution)/shard_map/ppermute | solution.py:22
  88.2 6.2 %collective-permute-start.12 = (f32[1,130,1]{2,1,0:T(8,128)S(1)}, f32[1,130,1]{2,1,0:T(8,128)S(1)}, u32[]{:S(2)}, u32[]{:S(2)}) collective-permute-start(f32[1,130,1]{2,1,0:T(8,128)S(1)} %get-tuple-element.18), channel_id=1, source_target_pairs={{2,0},{3,1},{6,4},{7,5},{10,8},{11,9},{14,12},{15,13},{18,16},{19,... | collective-permute-start | bytes 1568 | tf_op jit(solution)/shard_map/ppermute | solution.py:24
where the time goes:
time: 134 us
  blocking collectives  60.3 us (45%)
  waiting for transfers between devices  27.3 us (20%)
  starting transfers between devices  24.1 us (18%)
  other arithmetic  13.7 us (10%)
  between operations  6.7 us (5%)
  local copies, waits for them, and re-layouts  1.64 us (1%)
    psum x2, blocking collectives, inner_pair(): lax.psum((jnp.sum(resid_now * precond_now), jnp.sum(precond_now * image_n...  60.3 us
    ppermute x6, waiting for transfers between devices, extended(): lax.ppermute(head, axis, [((i + 1) % count, i) for i in range(ends)])  25.4 us
    ppermute x6, starting transfers between devices, extended(): lax.ppermute(tail, axis, [(i, (i + 1) % count) for i in range(ends)])  16.3 us
    ppermute x6, starting transfers between devices, extended(): lax.ppermute(head, axis, [((i + 1) % count, i) for i in range(ends)])  7.75 us
    add x1, other arithmetic, lookup(): cond + jnp.where(node_class == klass, class_conductance[:, klass][:, None...  6.45 us
    reduce_sum x2, other arithmetic, inner_pair(): jnp.sum(precond_now * image_now)  3.82 us
  transfers between devices with their start and end apart: 14, of which 9 were waited for; matrix products, arithmetic and copies ran while one was open for 0% of the time, Pallas kernels for 0%

commit v1 on v0

v1 whole, which is shorter than its diff:
```python
import functools

import jax
import jax.numpy as jnp
from jax import lax
from jax.experimental import pallas as pl
from jax.experimental.pallas import tpu as pltpu
from jax.sharding import PartitionSpec as P

MESH = pl.DeviceIdType.MESH
PAD = 8
SLAB = 8
via_conductance = 2.0
pad_conductance = 4.0
leakage = 0.05


def fold(x):
    parts = [x[:, k : k + 128] for k in range(0, x.shape[1], 128)]
    while len(parts) > 1:
        half = len(parts) // 2
        parts = [parts[k] + parts[k + half] for k in range(half)] + parts[2 * half :]
    return parts[0]


def kernel(sizes, cur_hbm, cls_hbm, table, pad_hbm, via_hbm, drop_hbm, res_hbm, worst_hbm,
           cur, cls, pad, via, cond, edge, inv, zed, zedq, wed, yed, yedq, ued, out,
           row_out, row_in, col_out, col_in, side, gather,
           load_sem, edge_send, edge_recv, layer_send, layer_recv, sum_send, sum_recv, store_sem):
    rows, cols, layers = sizes
    height, width = cur.shape
    me_r, me_c, me_l = lax.axis_index("row"), lax.axis_index("col"), lax.axis_index("layer")
    others = rows * cols * layers - 1
    slabs = height // SLAB

    def peer(k):
        r = lax.rem(me_r + k // (cols * layers), rows)
        c = lax.rem(me_c + lax.rem(k // layers, cols), cols)
        l = lax.rem(me_l + lax.rem(k, layers), layers)
        return {"row": r, "col": c, "layer": l}

    def each_peer(body):
        if others < 32:
            for k in range(1, others + 1):
                body(k)
        else:
            def step(k, carry):
                body(k)
                return carry
            lax.fori_loop(1, others + 1, step, 0)

    loads = [
        pltpu.make_async_copy(src, dst, load_sem.at[k])
        for k, (src, dst) in enumerate(
            ((cls_hbm.at[0], cls), (via_hbm, via), (pad_hbm.at[0], pad), (cur_hbm.at[0], cur))
        )
    ]
    for load in loads:
        load.start()

    barrier = pltpu.get_barrier_semaphore()
    each_peer(lambda k: pl.semaphore_signal(barrier, inc=1, device_id=peer(k), device_id_type=MESH))

    present = (me_r > 0, me_r < rows - 1, me_c > 0, me_c < cols - 1)
    exists = (rows > 1, rows > 1, cols > 1, cols > 1)
    target = ({"row": me_r - 1}, {"row": me_r + 1}, {"col": me_c - 1}, {"col": me_c + 1})

    def border(rnd, way):
        src = row_out if way < 2 else col_out
        dst = row_in if way < 2 else col_in
        return pltpu.make_async_remote_copy(
            src_ref=src.at[rnd, way % 2],
            dst_ref=dst.at[rnd, 1 - way % 2],
            send_sem=edge_send.at[rnd, way],
            recv_sem=edge_recv.at[rnd, way ^ 1],
            device_id=target[way],
            device_id_type=MESH,
        )

    def arrival(rnd, way):
        buf = row_in if way < 2 else col_in
        return pltpu.make_async_copy(
            buf.at[rnd, way % 2], buf.at[rnd, way % 2], edge_recv.at[rnd, way]
        )

    def send_borders(rnd, field):
        row_out[rnd, 0] = field[PAD : PAD + 1, :]
        row_out[rnd, 1] = field[PAD + height - 1 : PAD + height, :]
        for way in (0, 1):
            if exists[way]:
                pl.when(present[way])(lambda way=way: border(rnd, way).start())
        col_out[rnd, 0] = jnp.transpose(field[PAD : PAD + height, 0:128])[0:1, :]
        col_out[rnd, 1] = jnp.transpose(field[PAD : PAD + height, width - 128 : width])[127:128, :]
        for way in (2, 3):
            if exists[way]:
                pl.when(present[way])(lambda way=way: border(rnd, way).start())

    def take_borders(rnd, field):
        for way in range(4):
            if exists[way]:
                pl.when(present[way])(lambda way=way: arrival(rnd, way).wait())
        field[PAD - 1 : PAD, :] = row_in[rnd, 0]
        field[PAD + height : PAD + height + 1, :] = row_in[rnd, 1]
        for k in range(2):
            side[k] = jnp.transpose(jnp.broadcast_to(col_in[rnd, k], (128, height)))

    def clear(rnd):
        for way in range(4):
            buf = row_in if way < 2 else col_in
            def zero(buf=buf, way=way):
                buf[rnd, way % 2] = jnp.zeros(buf.shape[2:], jnp.float32)
            if exists[way]:
                pl.when(jnp.logical_not(present[way]))(zero)
            else:
                zero()

    for rnd in range(3):
        clear(rnd)

    lane = lax.broadcasted_iota(jnp.int32, (SLAB, 128), 1)

    def around(field, s):
        lo = PAD + s * SLAB
        here = field[lo : lo + SLAB, :]
        north = field[lo - 1 : lo + SLAB - 1, :]
        south = field[lo + 1 : lo + SLAB + 1, :]
        left, right = pltpu.roll(here, 1, 1), pltpu.roll(here, width - 1, 1)
        at = slice(s * SLAB, (s + 1) * SLAB)
        west = jnp.concatenate(
            [jnp.where(lane == 0, side[0, at, :], left[:, :128]), left[:, 128:]], axis=1)
        east = jnp.concatenate(
            [right[:, :-128], jnp.where(lane == 127, side[1, at, :], right[:, -128:])], axis=1)
        return here, (north, south, west, east)

    def to_partner(rnd, s):
        at = pl.ds(s * chunk, chunk)
        src = (zed, yed)[rnd].at[pl.ds(PAD + s * chunk, chunk)]
        return pltpu.make_async_remote_copy(
            src_ref=src, dst_ref=(zedq, yedq)[rnd].at[at],
            send_sem=layer_send.at[rnd, s], recv_sem=layer_recv.at[rnd, s],
            device_id={"layer": 1 - me_l}, device_id_type=MESH)

    chunks = layer_send.shape[1]
    chunk = height // chunks

    loads[0].wait()
    for s in range(slabs):
        at = slice(s * SLAB, (s + 1) * SLAB)
        klass = cls[at, :]
        value = jnp.full(klass.shape, table[0, 0], jnp.float32)
        for k in range(1, table.shape[1]):
            value = jnp.where(klass == k, table[0, k], value)
        cond[PAD + s * SLAB : PAD + (s + 1) * SLAB, :] = value

    pl.semaphore_wait(barrier, others)
    send_borders(0, cond)
    for load in loads[1:]:
        load.wait()
    take_borders(0, cond)

    for s in range(slabs):
        at = slice(s * SLAB, (s + 1) * SLAB)
        here, beside = around(cond, s)
        diagonal = via_conductance * via[at, :].astype(jnp.float32)
        diagonal = diagonal + pad_conductance * pad[at, :].astype(jnp.float32) + leakage
        for k in range(4):
            value = jnp.where(beside[k] > 0.0, 0.5 * (here + beside[k]), 0.0)
            edge[k, at, :] = value
            diagonal = diagonal + value
        recip = 1.0 / diagonal
        inv[at, :] = recip
        zed[PAD + s * SLAB : PAD + (s + 1) * SLAB, :] = cur[at, :] * recip
        if (s + 1) * SLAB % chunk == 0:
            to_partner(0, (s + 1) * SLAB // chunk - 1).start()
    send_borders(1, zed)

    def image(rnd, field, other, base, s):
        at = slice(s * SLAB, (s + 1) * SLAB)
        if s * SLAB % chunk == 0:
            to_partner(rnd, s * SLAB // chunk).wait_recv()
        here, beside = around(field, s)
        total = edge[0, at, :] * beside[0] + edge[1, at, :] * beside[1]
        total = total + (edge[2, at, :] * beside[2] + edge[3, at, :] * beside[3])
        cross = via_conductance * via[at, :].astype(jnp.float32) * other[at, :]
        return here, base - total - cross

    take_borders(1, zed)
    gamma = delta = eps = jnp.zeros((SLAB, 128), jnp.float32)
    for s in range(slabs):
        at = slice(s * SLAB, (s + 1) * SLAB)
        here, w = image(0, zed, zedq, cur[at, :], s)
        y = w * inv[at, :]
        wed[at, :] = w
        yed[PAD + s * SLAB : PAD + (s + 1) * SLAB, :] = y
        gamma = gamma + fold(cur[at, :] * here)
        delta = delta + fold(w * here)
        eps = eps + fold(w * y)
        if (s + 1) * SLAB % chunk == 0:
            to_partner(1, (s + 1) * SLAB // chunk - 1).start()
    send_borders(2, yed)

    eps_all = jnp.sum(eps, keepdims=True)
    delta_all = jnp.sum(delta, keepdims=True)
    a_d = jnp.where(eps_all > 0.0, delta_all / jnp.where(eps_all > 0.0, eps_all, 1.0), 0.0)

    take_borders(2, yed)
    s0 = s1 = t0 = t1 = t2 = jnp.zeros((SLAB, 128), jnp.float32)
    for s in range(slabs):
        at = slice(s * SLAB, (s + 1) * SLAB)
        w = wed[at, :]
        y, u = image(1, yed, yedq, w, s)
        ued[at, :] = u
        r1 = cur[at, :] - a_d * w
        z1 = zed[PAD + s * SLAB : PAD + (s + 1) * SLAB, :] - a_d * y
        w1 = w - a_d * u
        s0 = s0 + fold(r1 * z1)
        s1 = s1 + fold(w * z1)
        t0 = t0 + fold(z1 * w1)
        t1 = t1 + fold(z1 * u + y * w1)
        t2 = t2 + fold(y * u)

    packet = jnp.zeros((SLAB, 128), jnp.float32)
    for k, value in enumerate((gamma, delta, s0, s1, eps, t0, t1, t2)):
        packet = packet + jnp.where(lane == k, jnp.sum(value, axis=1, keepdims=True), 0.0)
    packet = jnp.sum(packet, axis=0, keepdims=True)
    packet = jnp.where(lane[0:1] == 8, a_d, packet)
    gather[0] = packet

    def share(k):
        return pltpu.make_async_remote_copy(
            src_ref=gather.at[0], dst_ref=gather.at[k], send_sem=sum_send, recv_sem=sum_recv,
            device_id=peer(k), device_id_type=MESH)

    each_peer(lambda k: share(k).start())
    everyone = gather.at[pl.ds(1, others)]
    pltpu.make_async_copy(everyone, everyone, sum_recv).wait()

    table_in = gather[...].reshape(others + 1, 128)
    lanes = lax.broadcasted_iota(jnp.int32, table_in.shape, 1)
    g, d, s0, s1, s2, t0, t1, t2, a_ds = (
        jnp.sum(jnp.where(lanes == k, table_in, 0.0), axis=1, keepdims=True) for k in range(9)
    )
    energy = jnp.sum(g, axis=0, keepdims=True)
    step = energy / jnp.sum(d, axis=0, keepdims=True)
    away = step - a_ds
    energy_next = jnp.sum(s0 - 2.0 * away * s1 + away * away * s2, axis=0, keepdims=True)
    curve = jnp.sum(t0 - away * t1 + away * away * t2, axis=0, keepdims=True)
    ratio = energy_next / energy
    step_next = energy_next / (curve - ratio * energy_next / step)

    stores = []
    for s in range(slabs):
        at = slice(s * SLAB, (s + 1) * SLAB)
        z = zed[PAD + s * SLAB : PAD + (s + 1) * SLAB, :]
        y = yed[PAD + s * SLAB : PAD + (s + 1) * SLAB, :]
        w = wed[at, :]
        first = step * z
        drop = first + step_next * ((z - step * y) + ratio * z)
        out[0, at, :] = drop
        out[1, at, :] = (cur[at, :] - step * w) - step_next * ((w - step * ued[at, :]) + ratio * w)
        out[2, at, :] = jnp.maximum(first, drop)
        if (s + 1) * SLAB % chunk == 0:
            c = (s + 1) * SLAB // chunk - 1
            for k, dst in enumerate((drop_hbm, res_hbm, worst_hbm)):
                store = pltpu.make_async_copy(
                    out.at[k, pl.ds(c * chunk, chunk)], dst.at[0, pl.ds(c * chunk, chunk)],
                    store_sem.at[k, c])
                store.start()
                stores.append(store)

    for rnd in range(3):
        for way in range(4):
            if exists[way]:
                pl.when(present[way])(lambda rnd=rnd, way=way: border(rnd, way).wait_send())
    for rnd in range(2):
        for c in range(chunks):
            to_partner(rnd, c).wait_send()
    pltpu.make_async_copy(everyone, everyone, sum_send).wait()
    for store in stores:
        store.wait()


def local(sizes, current, node_class, class_conductance, pad_mask, via_mask):
    _, height, width = current.shape
    f32 = jnp.float32
    chunks = 4
    full = lambda kind=f32: pltpu.VMEM((height, width), kind)
    tall = pltpu.VMEM((height + 2 * PAD, width), f32)
    anywhere = pl.BlockSpec(memory_space=pl.ANY)
    dma = pltpu.SemaphoreType.DMA
    return pl.pallas_call(
        functools.partial(kernel, sizes),
        out_shape=[jax.ShapeDtypeStruct(current.shape, f32)] * 3,
        in_specs=[anywhere, anywhere, pl.BlockSpec(memory_space=pltpu.SMEM), anywhere, anywhere],
        out_specs=[anywhere] * 3,
        scratch_shapes=[
            full(), full(jnp.int32), full(jnp.int32), full(jnp.int32),
            tall, pltpu.VMEM((4, height, width), f32), full(),
            tall, full(), full(), tall, full(), full(), pltpu.VMEM((3, height, width), f32),
            pltpu.VMEM((3, 2, 1, width), f32), pltpu.VMEM((3, 2, 1, width), f32),
            pltpu.VMEM((3, 2, 1, height), f32), pltpu.VMEM((3, 2, 1, height), f32),
            pltpu.VMEM((2, height, 128), f32),
            pltpu.VMEM((sizes[0] * sizes[1] * sizes[2], 1, 128), f32),
            dma((4,)), dma((3, 4)), dma((3, 4)), dma((2, chunks)), dma((2, chunks)),
            dma, dma, dma((3, chunks)),
        ],
        compiler_params=pltpu.CompilerParams(collective_id=0, has_side_effects=True),
    )(current, node_class, class_conductance, pad_mask, via_mask)


def solution(mesh):
    field = P("layer", ("scen", "row"), "col")
    sizes = tuple(mesh.shape[name] for name in ("row", "col", "layer"))
    return jax.shard_map(
        functools.partial(local, sizes),
        mesh=mesh,
        in_specs=(field, field, P("layer", None), field, P(("scen", "row"), "col")),
        out_specs=(field, field, field),
        check_vma=False,
    )
```

time: 134 us -> 27.4 us (0.20)
  blocking collectives: 60.3 us -> 0 us
  waiting for transfers between devices: 27.3 us -> 0 us
  starting transfers between devices: 24.1 us -> 0 us
  Pallas kernels: 0 us -> 22.6 us
  other arithmetic: 13.7 us -> 0 us
  between operations: 6.7 us -> 0.65 us
  local copies, waits for them, and re-layouts: 1.64 us -> 3.97 us
    psum x2 -> x0, blocking collectives: 60.3 us -> none  [inner_pair(): lax.psum((jnp.sum(resid_now * precond_now), jnp.sum(precond_now * image_n...]
    ppermute x14 -> x0, waiting for transfers between devices: 27.3 us -> none  [the longest x6 25.4 us: extended(): lax.ppermute(head, axis, [((i + 1) % count, i) for i in range(ends)])]
    ppermute x14 -> x0, starting transfers between devices: 24.1 us -> none  [the longest x6 16.3 us: extended(): lax.ppermute(tail, axis, [(i, (i + 1) % count) for i in range(ends)])]
    pallas_call x0 -> x1, Pallas kernels: none -> 22.6 us  [local(): pl.pallas_call(functools.partial(kernel, sizes), out_shape=[jax.ShapeDtyp...]
    add x1 -> x0, other arithmetic: 6.45 us -> none  [lookup(): cond + jnp.where(node_class == klass, class_conductance[:, klass][:, None...]
    unnamed x8 -> x7, local copies, waits for them, and re-layouts: 0.02 us -> 3.97 us
    reduce_sum x2 -> x0, other arithmetic: 3.82 us -> none  [inner_pair(): jnp.sum(precond_now * image_now)]
    max x1 -> x0, other arithmetic: 2.34 us -> none  [local(): jnp.maximum(worst_field, drop_field)]
  transfers between devices with their start and end apart: 14 -> 0, of which waited for: 9 -> 0; matrix products, arithmetic and copies ran while one was open for 0% -> 0% of each run, Pallas kernels for 0% -> 0%
where the time goes in v1:
time: 27.4 us; the launch traced here: 27.2 us
  Pallas kernels  22.6 us (82%)
  local copies, waits for them, and re-layouts  3.97 us (14%)
  between operations  0.65 us (2%)
    pallas_call x1, Pallas kernels, local(): pl.pallas_call(functools.partial(kernel, sizes), out_shape=[jax.ShapeDtyp...  22.6 us
    unnamed x7, local copies, waits for them, and re-layouts  3.97 us

profile of v1, /device:TPU:0, one launch (start us, length us, event | category | flops | bytes accessed | tf_op | source)
XLA Modules:
  0.0 27.2 jit_solution(1408401399532791835)
XLA Ops:
  0.6 22.6 %shard_map.76 = (f32[1,128,1024]{2,1,0:T(8,128)}, f32[1,128,1024]{2,1,0:T(8,128)}, f32[1,128,1024]{2,1,0:T(8,128)}) custom-call(f32[1,128,1024]{2,1,0:T(8,128)} %cur_hbm.1, s32[1,128,1024]{2,1,0:T(8,128)} %cls_hbm.1, f32[1,8]{1,0:T(1,128)} %table.1, s32[1,128,1024]{2,1,0:T(8,128)} %pad_hbm.1, s32[128,1024]{1,0:T(8,128)} %via_hbm.1), custom_call_target="tpu_custom_call" | custom-call | tf_op jit(solution)/shard_map/pallas_call | solution.py:291
  23.2 0.0 copy-start.1
  23.2 1.9 %copy.11 = f32[1,128,1024]{2,1,0:T(8,128)} copy(f32[1,128,1024]{2,1,0:T(8,128)} %get-tuple-element.6) | data formatting | bytes 1048576
  25.2 0.0 copy-done.1
  25.2 0.0 copy-start
  25.2 0.8 %copy.12 = f32[1,128,1024]{2,1,0:T(8,128)} copy(f32[1,128,1024]{2,1,0:T(8,128)S(1)} %copy-done.1) | data formatting | bytes 1048576
  26.0 0.4 %copy-done = f32[1,128,1024]{2,1,0:T(8,128)S(1)} copy-done((f32[1,128,1024]{2,1,0:T(8,128)S(1)}, f32[1,128,1024]{2,1,0:T(8,128)}, u32[]{:S(2)}) %copy-start) | copy-done | bytes 524312
  26.4 0.8 %copy.13 = f32[1,128,1024]{2,1,0:T(8,128)} copy(f32[1,128,1024]{2,1,0:T(8,128)S(1)} %copy-done) | data formatting | bytes 1048576
Async XLA Ops:
  23.2 2.0 %copy-start.1 = (f32[1,128,1024]{2,1,0:T(8,128)S(1)}, f32[1,128,1024]{2,1,0:T(8,128)}, u32[]{:S(2)}) copy-start(f32[1,128,1024]{2,1,0:T(8,128)} %get-tuple-element.7) | copy-start | bytes 1572868
  25.2 1.2 %copy-start = (f32[1,128,1024]{2,1,0:T(8,128)S(1)}, f32[1,128,1024]{2,1,0:T(8,128)}, u32[]{:S(2)}) copy-start(f32[1,128,1024]{2,1,0:T(8,128)} %get-tuple-element.8) | copy-start | bytes 1572868

commit v2 on v1

--- a/solution.py
+++ b/solution.py
@@ -23,10 +23,10 @@
     return parts[0]
 
 
-def kernel(sizes, cur_hbm, cls_hbm, table, pad_hbm, via_hbm, drop_hbm, res_hbm, worst_hbm,
-           cur, cls, pad, via, cond, edge, inv, zed, zedq, wed, yed, yedq, ued, out,
+def kernel(sizes, cur_hbm, cls_hbm, table, pad_hbm, via_hbm, cur, zed, wed, yed, ued, scal,
+           cls, pad, via, cond, edge, inv, zedq, yedq,
            row_out, row_in, col_out, col_in, side, gather,
-           load_sem, edge_send, edge_recv, layer_send, layer_recv, sum_send, sum_recv, store_sem):
+           load_sem, edge_send, edge_recv, layer_send, layer_recv, sum_send, sum_recv):
     rows, cols, layers = sizes
     height, width = cur.shape
     me_r, me_c, me_l = lax.axis_index("row"), lax.axis_index("col"), lax.axis_index("layer")
@@ -248,6 +248,25 @@
     ratio = energy_next / energy
     step_next = energy_next / (curve - ratio * energy_next / step)
 
+    for k, value in enumerate((step, step_next, ratio)):
+        scal[k : k + 1, :] = jnp.broadcast_to(value, (1, 128))
+
+    for rnd in range(3):
+        for way in range(4):
+            if exists[way]:
+                pl.when(present[way])(lambda rnd=rnd, way=way: border(rnd, way).wait_send())
+    for rnd in range(2):
+        for c in range(chunks):
+            to_partner(rnd, c).wait_send()
+    pltpu.make_async_copy(everyone, everyone, sum_send).wait()
+
+
+def finish(cur, zed, wed, yed, ued, scal, drop_hbm, res_hbm, worst_hbm, out, store_sem):
+    height = cur.shape[0]
+    slabs = height // SLAB
+    chunks = store_sem.shape[1]
+    chunk = height // chunks
+    step, step_next, ratio = (scal[k : k + 1, 0:1] for k in range(3))
     stores = []
     for s in range(slabs):
         at = slice(s * SLAB, (s + 1) * SLAB)
@@ -268,14 +287,6 @@
                 store.start()
                 stores.append(store)
 
-    for rnd in range(3):
-        for way in range(4):
-            if exists[way]:
-                pl.when(present[way])(lambda rnd=rnd, way=way: border(rnd, way).wait_send())
-    for rnd in range(2):
-        for c in range(chunks):
-            to_partner(rnd, c).wait_send()
-    pltpu.make_async_copy(everyone, everyone, sum_send).wait()
     for store in stores:
         store.wait()
 
@@ -288,24 +299,34 @@
     tall = pltpu.VMEM((height + 2 * PAD, width), f32)
     anywhere = pl.BlockSpec(memory_space=pl.ANY)
     dma = pltpu.SemaphoreType.DMA
-    return pl.pallas_call(
+    kept = [(height, width), tall.shape, (height, width), tall.shape, (height, width), (8, 128)]
+    far = pl.BlockSpec(memory_space=pltpu.HBM)
+    inside = pl.BlockSpec(memory_space=pltpu.VMEM)
+    fields = pl.pallas_call(
         functools.partial(kernel, sizes),
-        out_shape=[jax.ShapeDtypeStruct(current.shape, f32)] * 3,
-        in_specs=[anywhere, anywhere, pl.BlockSpec(memory_space=pltpu.SMEM), anywhere, anywhere],
-        out_specs=[anywhere] * 3,
+        out_shape=[pltpu.VMEM(shape, f32) for shape in kept],
+        in_specs=[far, far, pl.BlockSpec(memory_space=pltpu.SMEM), far, far],
+        out_specs=[inside] * len(kept),
         scratch_shapes=[
-            full(), full(jnp.int32), full(jnp.int32), full(jnp.int32),
-            tall, pltpu.VMEM((4, height, width), f32), full(),
-            tall, full(), full(), tall, full(), full(), pltpu.VMEM((3, height, width), f32),
+            full(jnp.int32), full(jnp.int32), full(jnp.int32),
+            tall, pltpu.VMEM((4, height, width), f32), full(), full(), full(),
             pltpu.VMEM((3, 2, 1, width), f32), pltpu.VMEM((3, 2, 1, width), f32),
             pltpu.VMEM((3, 2, 1, height), f32), pltpu.VMEM((3, 2, 1, height), f32),
             pltpu.VMEM((2, height, 128), f32),
             pltpu.VMEM((sizes[0] * sizes[1] * sizes[2], 1, 128), f32),
-            dma((4,)), dma((3, 4)), dma((3, 4)), dma((2, chunks)), dma((2, chunks)),
-            dma, dma, dma((3, chunks)),
+            dma((4,)), dma((3, 4)), dma((3, 4)), dma((2, chunks)), dma((2, chunks)), dma, dma,
         ],
-        compiler_params=pltpu.CompilerParams(collective_id=0, has_side_effects=True),
+        compiler_params=pltpu.CompilerParams(
+            collective_id=0, has_side_effects=True, vmem_limit_bytes=56 * 2**20),
     )(current, node_class, class_conductance, pad_mask, via_mask)
+    return pl.pallas_call(
+        finish,
+        out_shape=[jax.ShapeDtypeStruct(current.shape, f32)] * 3,
+        in_specs=[inside] * len(kept),
+        out_specs=[anywhere] * 3,
+        scratch_shapes=[pltpu.VMEM((3, height, width), f32), dma((3, chunks))],
+        compiler_params=pltpu.CompilerParams(vmem_limit_bytes=8 * 2**20),
+    )(*fields)
 
 
 def solution(mesh):

time: 27.4 us -> 23.4 us (0.85)
  local copies, waits for them, and re-layouts: 3.97 us -> 0 us
    unnamed x7 -> x0, local copies, waits for them, and re-layouts: 3.97 us -> none
    pallas_call x1 -> x2, Pallas kernels: 22.6 us -> 22.6 us  [the longest x1 21.3 us: local(): pl.pallas_call(functools.partial(kernel, sizes), out_shape=[pltpu.VMEM(sh...]
where the time goes in v2:
time: 23.4 us; the launch traced here: 23.2 us
  Pallas kernels  22.6 us (97%)
  between operations  0.64 us (3%)
    pallas_call x1, Pallas kernels, local(): pl.pallas_call(functools.partial(kernel, sizes), out_shape=[pltpu.VMEM(sh...  21.3 us
    pallas_call x1, Pallas kernels, local(): pl.pallas_call(finish, out_shape=[jax.ShapeDtypeStruct(current.shape, f32...  1.34 us

profile of v2, /device:TPU:0, one launch (start us, length us, event | category | flops | bytes accessed | tf_op | source)
XLA Modules:
  0.0 23.2 jit_solution(6532722932842591202)
XLA Ops:
  0.6 21.3 %shard_map.76 = (f32[128,1024]{1,0:T(8,128)S(1)}, f32[144,1024]{1,0:T(8,128)S(1)}, f32[128,1024]{1,0:T(8,128)S(1)}, f32[144,1024]{1,0:T(8,128)S(1)}, f32[128,1024]{1,0:T(8,128)S(1)}, /*index=5*/f32[8,128]{1,0:T(8,128)S(1)}) custom-call(f32[1,128,1024]{2,1,0:T(8,128)} %cur_hbm.1, s32[1,128,1024]{2,1,0:T(8,128)} %cls_hbm.1, f32[1,8]{1,0:T(1,128)} %table.1, ...), custom_call_target="tpu_custom_call" | custom-call | tf_op jit(solution)/shard_map/pallas_call | solution.py:305
  21.9 1.3 %shard_map.77 = (f32[1,128,1024]{2,1,0:T(8,128)}, f32[1,128,1024]{2,1,0:T(8,128)}, f32[1,128,1024]{2,1,0:T(8,128)}) custom-call(f32[128,1024]{1,0:T(8,128)S(1)} %get-tuple-element.9.cur, f32[144,1024]{1,0:T(8,128)S(1)} %get-tuple-element.10.zed, f32[128,1024]{1,0:T(8,128)S(1)} %get-tuple-element.11.wed, f32[144,1024]{1,0:T(8,128)S(1)} %get-tuple-element.12.yed, ...), custom_call_target="tpu_custom_call" | custom-call | tf_op jit(solution)/shard_map/pallas_call | solution.py:322

commit v3 on v2

--- a/solution.py
+++ b/solution.py
@@ -59,7 +59,27 @@
         load.start()
 
     barrier = pltpu.get_barrier_semaphore()
-    each_peer(lambda k: pl.semaphore_signal(barrier, inc=1, device_id=peer(k), device_id_type=MESH))
+    def greet(k):
+        pl.semaphore_signal(barrier, inc=1, device_id=peer(k), device_id_type=MESH)
+
+    if rows <= 4:
+        plane = cols * layers
+        for k in range(1, plane):
+            greet(k)
+        for way, row in ((0, me_r - 1), (1, me_r + 1)):
+            def beyond(row=row):
+                for k in range(plane):
+                    c = lax.rem(me_c + k // layers, cols)
+                    l = lax.rem(me_l + k % layers, layers)
+                    pl.semaphore_signal(barrier, inc=1, device_id={"row": row, "col": c, "layer": l},
+                                        device_id_type=MESH)
+            if rows > 1:
+                pl.when((me_r > 0, me_r < rows - 1)[way])(beyond)
+        sides = 1 + (me_r > 0).astype(jnp.int32) + (me_r < rows - 1).astype(jnp.int32)
+        greeted = sides * plane - 1
+    else:
+        each_peer(greet)
+        greeted = others
 
     present = (me_r > 0, me_r < rows - 1, me_c > 0, me_c < cols - 1)
     exists = (rows > 1, rows > 1, cols > 1, cols > 1)
@@ -119,29 +139,44 @@
 
     lane = lax.broadcasted_iota(jnp.int32, (SLAB, 128), 1)
 
-    def around(field, s):
-        lo = PAD + s * SLAB
-        here = field[lo : lo + SLAB, :]
-        north = field[lo - 1 : lo + SLAB - 1, :]
-        south = field[lo + 1 : lo + SLAB + 1, :]
-        left, right = pltpu.roll(here, 1, 1), pltpu.roll(here, width - 1, 1)
-        at = slice(s * SLAB, (s + 1) * SLAB)
-        west = jnp.concatenate(
-            [jnp.where(lane == 0, side[0, at, :], left[:, :128]), left[:, 128:]], axis=1)
-        east = jnp.concatenate(
-            [right[:, :-128], jnp.where(lane == 127, side[1, at, :], right[:, -128:])], axis=1)
+    inner = (128, width - 128)
+    middle = [(s, *inner) for s in range(1, slabs - 1)]
+    rim = [(0, 0, width), (slabs - 1, 0, width)]
+    rim += [(s, lo, hi) for s in range(1, slabs - 1) for lo, hi in ((0, 128), (width - 128, width))]
+
+    def around(field, piece):
+        s, lo, hi = piece
+        top = PAD + s * SLAB
+        at = slice(s * SLAB, (s + 1) * SLAB)
+        north = field[top - 1 : top + SLAB - 1, lo:hi]
+        south = field[top + 1 : top + SLAB + 1, lo:hi]
+        first, last = max(lo - 128, 0), min(hi + 128, width)
+        wide = field[top : top + SLAB, first:last]
+        here = wide[:, lo - first : hi - first]
+        west = pltpu.roll(wide, 1, 1)[:, lo - first : hi - first]
+        east = pltpu.roll(wide, last - first - 1, 1)[:, lo - first : hi - first]
+        if lo == 0:
+            edge_tile = jnp.where(lane == 0, side[0, at, :], west[:, :128])
+            west = edge_tile if hi == 128 else jnp.concatenate([edge_tile, west[:, 128:]], axis=1)
+        if hi == width:
+            edge_tile = jnp.where(lane == 127, side[1, at, :], east[:, -128:])
+            east = edge_tile if hi - lo == 128 else jnp.concatenate([east[:, :-128], edge_tile], axis=1)
         return here, (north, south, west, east)
 
-    def to_partner(rnd, s):
-        at = pl.ds(s * chunk, chunk)
-        src = (zed, yed)[rnd].at[pl.ds(PAD + s * chunk, chunk)]
+    blocks = (
+        (SLAB, height - SLAB, *inner),
+        (0, SLAB, 0, width), (height - SLAB, height, 0, width),
+        (SLAB, height - SLAB, 0, 128), (SLAB, height - SLAB, width - 128, width),
+    )
+
+    def to_partner(rnd, b):
+        top, bottom, lo, hi = blocks[b]
+        src = (zed, yed)[rnd].at[pl.ds(PAD + top, bottom - top), pl.ds(lo, hi - lo)]
+        dst = (zedq, yedq)[rnd].at[pl.ds(top, bottom - top), pl.ds(lo, hi - lo)]
         return pltpu.make_async_remote_copy(
-            src_ref=src, dst_ref=(zedq, yedq)[rnd].at[at],
-            send_sem=layer_send.at[rnd, s], recv_sem=layer_recv.at[rnd, s],
+            src_ref=src, dst_ref=dst,
+            send_sem=layer_send.at[rnd, b], recv_sem=layer_recv.at[rnd, b],
             device_id={"layer": 1 - me_l}, device_id_type=MESH)
-
-    chunks = layer_send.shape[1]
-    chunk = height // chunks
 
     loads[0].wait()
     for s in range(slabs):
@@ -152,72 +187,96 @@
             value = jnp.where(klass == k, table[0, k], value)
         cond[PAD + s * SLAB : PAD + (s + 1) * SLAB, :] = value
 
-    pl.semaphore_wait(barrier, others)
+    pl.semaphore_wait(barrier, greeted)
     send_borders(0, cond)
     for load in loads[1:]:
         load.wait()
-    take_borders(0, cond)
-
-    for s in range(slabs):
-        at = slice(s * SLAB, (s + 1) * SLAB)
-        here, beside = around(cond, s)
-        diagonal = via_conductance * via[at, :].astype(jnp.float32)
-        diagonal = diagonal + pad_conductance * pad[at, :].astype(jnp.float32) + leakage
+
+    def setup(piece):
+        s, lo, hi = piece
+        at = slice(s * SLAB, (s + 1) * SLAB)
+        here, beside = around(cond, piece)
+        diagonal = via_conductance * via[at, lo:hi].astype(jnp.float32)
+        diagonal = diagonal + pad_conductance * pad[at, lo:hi].astype(jnp.float32) + leakage
         for k in range(4):
             value = jnp.where(beside[k] > 0.0, 0.5 * (here + beside[k]), 0.0)
-            edge[k, at, :] = value
+            edge[k, at, lo:hi] = value
             diagonal = diagonal + value
         recip = 1.0 / diagonal
-        inv[at, :] = recip
-        zed[PAD + s * SLAB : PAD + (s + 1) * SLAB, :] = cur[at, :] * recip
-        if (s + 1) * SLAB % chunk == 0:
-            to_partner(0, (s + 1) * SLAB // chunk - 1).start()
-    send_borders(1, zed)
-
-    def image(rnd, field, other, base, s):
-        at = slice(s * SLAB, (s + 1) * SLAB)
-        if s * SLAB % chunk == 0:
-            to_partner(rnd, s * SLAB // chunk).wait_recv()
-        here, beside = around(field, s)
-        total = edge[0, at, :] * beside[0] + edge[1, at, :] * beside[1]
-        total = total + (edge[2, at, :] * beside[2] + edge[3, at, :] * beside[3])
-        cross = via_conductance * via[at, :].astype(jnp.float32) * other[at, :]
+        inv[at, lo:hi] = recip
+        zed[PAD + s * SLAB : PAD + (s + 1) * SLAB, lo:hi] = cur[at, lo:hi] * recip
+
+    def image(field, other, base, piece):
+        s, lo, hi = piece
+        at = slice(s * SLAB, (s + 1) * SLAB)
+        here, beside = around(field, piece)
+        total = edge[0, at, lo:hi] * beside[0] + edge[1, at, lo:hi] * beside[1]
+        total = total + (edge[2, at, lo:hi] * beside[2] + edge[3, at, lo:hi] * beside[3])
+        cross = via_conductance * via[at, lo:hi].astype(jnp.float32) * other[at, lo:hi]
         return here, base - total - cross
 
-    take_borders(1, zed)
-    gamma = delta = eps = jnp.zeros((SLAB, 128), jnp.float32)
-    for s in range(slabs):
-        at = slice(s * SLAB, (s + 1) * SLAB)
-        here, w = image(0, zed, zedq, cur[at, :], s)
-        y = w * inv[at, :]
-        wed[at, :] = w
-        yed[PAD + s * SLAB : PAD + (s + 1) * SLAB, :] = y
-        gamma = gamma + fold(cur[at, :] * here)
-        delta = delta + fold(w * here)
-        eps = eps + fold(w * y)
-        if (s + 1) * SLAB % chunk == 0:
-            to_partner(1, (s + 1) * SLAB // chunk - 1).start()
-    send_borders(2, yed)
+    def ahead(sums, piece):
+        s, lo, hi = piece
+        at = slice(s * SLAB, (s + 1) * SLAB)
+        base = cur[at, lo:hi]
+        here, w = image(zed, zedq, base, piece)
+        y = w * inv[at, lo:hi]
+        wed[at, lo:hi] = w
+        yed[PAD + s * SLAB : PAD + (s + 1) * SLAB, lo:hi] = y
+        terms = (base * here, w * here, w * y)
+        return tuple(total + fold(term) for total, term in zip(sums, terms))
+
+    def depart(rnd, field):
+        send_borders(rnd + 1, field)
+        for b in range(1, len(blocks)):
+            to_partner(rnd, b).start()
+
+    def meanwhile(rnd, work, sums):
+        to_partner(rnd, 0).wait_recv()
+        for piece in middle:
+            sums = work(sums, piece)
+        return sums
+
+    def arrive(rnd, field, work, sums):
+        take_borders(rnd + 1, field)
+        for b in range(1, len(blocks)):
+            to_partner(rnd, b).wait_recv()
+        for piece in rim:
+            sums = work(sums, piece)
+        return sums
+
+    for piece in middle:
+        setup(piece)
+    to_partner(0, 0).start()
+    take_borders(0, cond)
+    for piece in rim:
+        setup(piece)
+
+    nothing = jnp.zeros((SLAB, 128), jnp.float32)
+    depart(0, zed)
+    sums = meanwhile(0, ahead, (nothing,) * 3)
+    to_partner(1, 0).start()
+    gamma, delta, eps = arrive(0, zed, ahead, sums)
+    depart(1, yed)
 
     eps_all = jnp.sum(eps, keepdims=True)
     delta_all = jnp.sum(delta, keepdims=True)
     a_d = jnp.where(eps_all > 0.0, delta_all / jnp.where(eps_all > 0.0, eps_all, 1.0), 0.0)
 
-    take_borders(2, yed)
-    s0 = s1 = t0 = t1 = t2 = jnp.zeros((SLAB, 128), jnp.float32)
-    for s in range(slabs):
-        at = slice(s * SLAB, (s + 1) * SLAB)
-        w = wed[at, :]
-        y, u = image(1, yed, yedq, w, s)
-        ued[at, :] = u
-        r1 = cur[at, :] - a_d * w
-        z1 = zed[PAD + s * SLAB : PAD + (s + 1) * SLAB, :] - a_d * y
+    def again(sums, piece):
+        s, lo, hi = piece
+        at = slice(s * SLAB, (s + 1) * SLAB)
+        w = wed[at, lo:hi]
+        y, u = image(yed, yedq, w, piece)
+        ued[at, lo:hi] = u
+        r1 = cur[at, lo:hi] - a_d * w
+        z1 = zed[PAD + s * SLAB : PAD + (s + 1) * SLAB, lo:hi] - a_d * y
         w1 = w - a_d * u
-        s0 = s0 + fold(r1 * z1)
-        s1 = s1 + fold(w * z1)
-        t0 = t0 + fold(z1 * w1)
-        t1 = t1 + fold(z1 * u + y * w1)
-        t2 = t2 + fold(y * u)
+        terms = (r1 * z1, w * z1, z1 * w1, z1 * u + y * w1, y * u)
+        return tuple(total + fold(term) for total, term in zip(sums, terms))
+
+    sums = meanwhile(1, again, (nothing,) * 5)
+    s0, s1, t0, t1, t2 = arrive(1, yed, again, sums)
 
     packet = jnp.zeros((SLAB, 128), jnp.float32)
     for k, value in enumerate((gamma, delta, s0, s1, eps, t0, t1, t2)):
@@ -256,8 +315,8 @@
             if exists[way]:
                 pl.when(present[way])(lambda rnd=rnd, way=way: border(rnd, way).wait_send())
     for rnd in range(2):
-        for c in range(chunks):
-            to_partner(rnd, c).wait_send()
+        for b in range(len(blocks)):
+            to_partner(rnd, b).wait_send()
     pltpu.make_async_copy(everyone, everyone, sum_send).wait()
 
 
@@ -314,7 +373,7 @@
             pltpu.VMEM((3, 2, 1, height), f32), pltpu.VMEM((3, 2, 1, height), f32),
             pltpu.VMEM((2, height, 128), f32),
             pltpu.VMEM((sizes[0] * sizes[1] * sizes[2], 1, 128), f32),
-            dma((4,)), dma((3, 4)), dma((3, 4)), dma((2, chunks)), dma((2, chunks)), dma, dma,
+            dma((4,)), dma((3, 4)), dma((3, 4)), dma((2, 5)), dma((2, 5)), dma, dma,
         ],
         compiler_params=pltpu.CompilerParams(
             collective_id=0, has_side_effects=True, vmem_limit_bytes=56 * 2**20),

time: 23.4 us -> 21.2 us (0.906)
  Pallas kernels: 22.6 us -> 20.4 us
    pallas_call x1, Pallas kernels: 21.3 us -> 19.1 us  [local(): pl.pallas_call(functools.partial(kernel, sizes), out_shape=[pltpu.VMEM(sh...]
where the time goes in v3:
time: 21.2 us; the launch traced here: 21.1 us
  Pallas kernels  20.4 us (96%)
  between operations  0.64 us (3%)
    pallas_call x1, Pallas kernels, local(): pl.pallas_call(functools.partial(kernel, sizes), out_shape=[pltpu.VMEM(sh...  19.1 us
    pallas_call x1, Pallas kernels, local(): pl.pallas_call(finish, out_shape=[jax.ShapeDtypeStruct(current.shape, f32...  1.34 us

profile of v3, /device:TPU:0, one launch (start us, length us, event | category | flops | bytes accessed | tf_op | source)
XLA Modules:
  0.0 21.1 jit_solution(16412940176110269765)
XLA Ops:
  0.6 19.1 %shard_map.76 = (f32[128,1024]{1,0:T(8,128)S(1)}, f32[144,1024]{1,0:T(8,128)S(1)}, f32[128,1024]{1,0:T(8,128)S(1)}, f32[144,1024]{1,0:T(8,128)S(1)}, f32[128,1024]{1,0:T(8,128)S(1)}, /*index=5*/f32[8,128]{1,0:T(8,128)S(1)}) custom-call(f32[1,128,1024]{2,1,0:T(8,128)} %cur_hbm.1, s32[1,128,1024]{2,1,0:T(8,128)} %cls_hbm.1, f32[1,8]{1,0:T(1,128)} %table.1, ...), custom_call_target="tpu_custom_call" | custom-call | tf_op jit(solution)/shard_map/pallas_call | solution.py:364
  19.7 1.3 %shard_map.77 = (f32[1,128,1024]{2,1,0:T(8,128)}, f32[1,128,1024]{2,1,0:T(8,128)}, f32[1,128,1024]{2,1,0:T(8,128)}) custom-call(f32[128,1024]{1,0:T(8,128)S(1)} %get-tuple-element.9.cur, f32[144,1024]{1,0:T(8,128)S(1)} %get-tuple-element.10.zed, f32[128,1024]{1,0:T(8,128)S(1)} %get-tuple-element.11.wed, f32[144,1024]{1,0:T(8,128)S(1)} %get-tuple-element.12.yed, ...), custom_call_target="tpu_custom_call" | custom-call | tf_op jit(solution)/shard_map/pallas_call | solution.py:381

commit v4 on v3

--- a/solution.py
+++ b/solution.py
@@ -49,37 +49,57 @@
                 return carry
             lax.fori_loop(1, others + 1, step, 0)
 
+    inner = (128, width - 128)
+    middle = [(s, *inner) for s in range(1, slabs - 1)]
+    rim = [(0, 0, width), (slabs - 1, 0, width)]
+    rim += [(s, lo, hi) for s in range(1, slabs - 1) for lo, hi in ((0, 128), (width - 128, width))]
+
+    blocks = (
+        (SLAB, height - SLAB, *inner),
+        (0, SLAB, 0, width), (height - SLAB, height, 0, width),
+        (SLAB, height - SLAB, 0, 128), (SLAB, height - SLAB, width - 128, width),
+    )
+
+    def load_class(b):
+        top, bottom, lo, hi = blocks[b]
+        return pltpu.make_async_copy(
+            cls_hbm.at[0, pl.ds(top, bottom - top), pl.ds(lo, hi - lo)],
+            cls.at[pl.ds(top, bottom - top), pl.ds(lo, hi - lo)], load_sem.at[3 + b])
+
     loads = [
         pltpu.make_async_copy(src, dst, load_sem.at[k])
         for k, (src, dst) in enumerate(
-            ((cls_hbm.at[0], cls), (via_hbm, via), (pad_hbm.at[0], pad), (cur_hbm.at[0], cur))
-        )
+            ((via_hbm, via), (pad_hbm.at[0], pad), (cur_hbm.at[0], cur)))
     ]
-    for load in loads:
-        load.start()
-
+    for b in (1, 2, 3, 4, 0):
+        load_class(b).start()
     barrier = pltpu.get_barrier_semaphore()
     def greet(k):
         pl.semaphore_signal(barrier, inc=1, device_id=peer(k), device_id_type=MESH)
 
-    if rows <= 4:
-        plane = cols * layers
-        for k in range(1, plane):
+    if rows + cols <= 6:
+        for k in range(1, layers):
             greet(k)
-        for way, row in ((0, me_r - 1), (1, me_r + 1)):
-            def beyond(row=row):
-                for k in range(plane):
-                    c = lax.rem(me_c + k // layers, cols)
-                    l = lax.rem(me_l + k % layers, layers)
-                    pl.semaphore_signal(barrier, inc=1, device_id={"row": row, "col": c, "layer": l},
+        greeted = layers - 1
+        near = (
+            ("row", me_r - 1, me_r > 0), ("row", me_r + 1, me_r < rows - 1),
+            ("col", me_c - 1, me_c > 0), ("col", me_c + 1, me_c < cols - 1),
+        )
+        for axis, there, is_there in near:
+            def beyond(axis=axis, there=there):
+                for k in range(layers):
+                    l = lax.rem(me_l + k, layers)
+                    pl.semaphore_signal(barrier, inc=1, device_id={axis: there, "layer": l},
                                         device_id_type=MESH)
-            if rows > 1:
-                pl.when((me_r > 0, me_r < rows - 1)[way])(beyond)
-        sides = 1 + (me_r > 0).astype(jnp.int32) + (me_r < rows - 1).astype(jnp.int32)
-        greeted = sides * plane - 1
+            if (rows if axis == "row" else cols) > 1:
+                pl.when(is_there)(beyond)
+                greeted = greeted + layers * is_there.astype(jnp.int32)
     else:
         each_peer(greet)
         greeted = others
+
+    for load in loads:
+        load.start()
 
     present = (me_r > 0, me_r < rows - 1, me_c > 0, me_c < cols - 1)
     exists = (rows > 1, rows > 1, cols > 1, cols > 1)
@@ -138,11 +158,6 @@
         clear(rnd)
 
     lane = lax.broadcasted_iota(jnp.int32, (SLAB, 128), 1)
-
-    inner = (128, width - 128)
-    middle = [(s, *inner) for s in range(1, slabs - 1)]
-    rim = [(0, 0, width), (slabs - 1, 0, width)]
-    rim += [(s, lo, hi) for s in range(1, slabs - 1) for lo, hi in ((0, 128), (width - 128, width))]
 
     def around(field, piece):
         s, lo, hi = piece
@@ -163,12 +178,6 @@
             east = edge_tile if hi - lo == 128 else jnp.concatenate([east[:, :-128], edge_tile], axis=1)
         return here, (north, south, west, east)
 
-    blocks = (
-        (SLAB, height - SLAB, *inner),
-        (0, SLAB, 0, width), (height - SLAB, height, 0, width),
-        (SLAB, height - SLAB, 0, 128), (SLAB, height - SLAB, width - 128, width),
-    )
-
     def to_partner(rnd, b):
         top, bottom, lo, hi = blocks[b]
         src = (zed, yed)[rnd].at[pl.ds(PAD + top, bottom - top), pl.ds(lo, hi - lo)]
@@ -178,18 +187,24 @@
             send_sem=layer_send.at[rnd, b], recv_sem=layer_recv.at[rnd, b],
             device_id={"layer": 1 - me_l}, device_id_type=MESH)
 
-    loads[0].wait()
-    for s in range(slabs):
-        at = slice(s * SLAB, (s + 1) * SLAB)
-        klass = cls[at, :]
+    def lookup(piece):
+        s, lo, hi = piece
+        klass = cls[s * SLAB : (s + 1) * SLAB, lo:hi]
         value = jnp.full(klass.shape, table[0, 0], jnp.float32)
         for k in range(1, table.shape[1]):
             value = jnp.where(klass == k, table[0, k], value)
-        cond[PAD + s * SLAB : PAD + (s + 1) * SLAB, :] = value
-
+        cond[PAD + s * SLAB : PAD + (s + 1) * SLAB, lo:hi] = value
+
+    for b in range(1, len(blocks)):
+        load_class(b).wait()
+    for piece in rim:
+        lookup(piece)
     pl.semaphore_wait(barrier, greeted)
     send_borders(0, cond)
-    for load in loads[1:]:
+    load_class(0).wait()
+    for piece in middle:
+        lookup(piece)
+    for load in loads:
         load.wait()
 
     def setup(piece):
@@ -353,7 +368,7 @@
 def local(sizes, current, node_class, class_conductance, pad_mask, via_mask):
     _, height, width = current.shape
     f32 = jnp.float32
-    chunks = 4
+    chunks = 8
     full = lambda kind=f32: pltpu.VMEM((height, width), kind)
     tall = pltpu.VMEM((height + 2 * PAD, width), f32)
     anywhere = pl.BlockSpec(memory_space=pl.ANY)
@@ -373,7 +388,7 @@
             pltpu.VMEM((3, 2, 1, height), f32), pltpu.VMEM((3, 2, 1, height), f32),
             pltpu.VMEM((2, height, 128), f32),
             pltpu.VMEM((sizes[0] * sizes[1] * sizes[2], 1, 128), f32),
-            dma((4,)), dma((3, 4)), dma((3, 4)), dma((2, 5)), dma((2, 5)), dma, dma,
+            dma((8,)), dma((3, 4)), dma((3, 4)), dma((2, 5)), dma((2, 5)), dma, dma,
         ],
         compiler_params=pltpu.CompilerParams(
             collective_id=0, has_side_effects=True, vmem_limit_bytes=56 * 2**20),

time: 21.2 us -> 21.3 us (level)
  no operation moved by 1% of the time
where the time goes in v4:
time: 21.3 us; the launch traced here: 21.1 us
  Pallas kernels  20.5 us (96%)
  between operations  0.64 us (3%)
    pallas_call x1, Pallas kernels, local(): pl.pallas_call(functools.partial(kernel, sizes), out_shape=[pltpu.VMEM(sh...  19.1 us
    pallas_call x1, Pallas kernels, local(): pl.pallas_call(finish, out_shape=[jax.ShapeDtypeStruct(current.shape, f32...  1.4 us

profile of v4, /device:TPU:0, one launch (start us, length us, event | category | flops | bytes accessed | tf_op | source)
XLA Modules:
  0.0 21.1 jit_solution(205780940621939105)
XLA Ops:
  0.6 19.1 %shard_map.76 = (f32[128,1024]{1,0:T(8,128)S(1)}, f32[144,1024]{1,0:T(8,128)S(1)}, f32[128,1024]{1,0:T(8,128)S(1)}, f32[144,1024]{1,0:T(8,128)S(1)}, f32[128,1024]{1,0:T(8,128)S(1)}, /*index=5*/f32[8,128]{1,0:T(8,128)S(1)}) custom-call(f32[1,128,1024]{2,1,0:T(8,128)} %cur_hbm.1, s32[1,128,1024]{2,1,0:T(8,128)} %cls_hbm.1, f32[1,8]{1,0:T(1,128)} %table.1, ...), custom_call_target="tpu_custom_call" | custom-call | tf_op jit(solution)/shard_map/pallas_call | solution.py:379
  19.7 1.4 %shard_map.77 = (f32[1,128,1024]{2,1,0:T(8,128)}, f32[1,128,1024]{2,1,0:T(8,128)}, f32[1,128,1024]{2,1,0:T(8,128)}) custom-call(f32[128,1024]{1,0:T(8,128)S(1)} %get-tuple-element.9.cur, f32[144,1024]{1,0:T(8,128)S(1)} %get-tuple-element.10.zed, f32[128,1024]{1,0:T(8,128)S(1)} %get-tuple-element.11.wed, f32[144,1024]{1,0:T(8,128)S(1)} %get-tuple-element.12.yed, ...), custom_call_target="tpu_custom_call" | custom-call | tf_op jit(solution)/shard_map/pallas_call | solution.py:396

commit v5 on v4

--- a/solution.py
+++ b/solution.py
@@ -129,11 +129,13 @@
         for way in (0, 1):
             if exists[way]:
                 pl.when(present[way])(lambda way=way: border(rnd, way).start())
-        col_out[rnd, 0] = jnp.transpose(field[PAD : PAD + height, 0:128])[0:1, :]
-        col_out[rnd, 1] = jnp.transpose(field[PAD : PAD + height, width - 128 : width])[127:128, :]
-        for way in (2, 3):
+        for way, lo, lane_at in ((2, 0, 0), (3, width - 128, 127)):
+            def turn(way=way, lo=lo, lane_at=lane_at):
+                column = jnp.transpose(field[PAD : PAD + height, lo : lo + 128])
+                col_out[rnd, way - 2] = column[lane_at : lane_at + 1, :]
+                border(rnd, way).start()
             if exists[way]:
-                pl.when(present[way])(lambda way=way: border(rnd, way).start())
+                pl.when(present[way])(turn)
 
     def take_borders(rnd, field):
         for way in range(4):
@@ -142,7 +144,10 @@
         field[PAD - 1 : PAD, :] = row_in[rnd, 0]
         field[PAD + height : PAD + height + 1, :] = row_in[rnd, 1]
         for k in range(2):
-            side[k] = jnp.transpose(jnp.broadcast_to(col_in[rnd, k], (128, height)))
+            def turn(k=k):
+                side[k] = jnp.transpose(jnp.broadcast_to(col_in[rnd, k], (128, height)))
+            if exists[2 + k]:
+                pl.when(present[2 + k])(turn)
 
     def clear(rnd):
         for way in range(4):
@@ -156,6 +161,8 @@
 
     for rnd in range(3):
         clear(rnd)
+    for k in range(2):
+        side[k] = jnp.zeros(side.shape[1:], jnp.float32)
 
     lane = lax.broadcasted_iota(jnp.int32, (SLAB, 128), 1)
 
@@ -368,7 +375,7 @@
 def local(sizes, current, node_class, class_conductance, pad_mask, via_mask):
     _, height, width = current.shape
     f32 = jnp.float32
-    chunks = 8
+    chunks = 4
     full = lambda kind=f32: pltpu.VMEM((height, width), kind)
     tall = pltpu.VMEM((height + 2 * PAD, width), f32)
     anywhere = pl.BlockSpec(memory_space=pl.ANY)

time: 21.3 us -> 21.2 us (level)
  no operation moved by 1% of the time
where the time goes in v5:
time: 21.2 us; the launch traced here: 21.1 us
  Pallas kernels  20.4 us (96%)
  between operations  0.64 us (3%)
    pallas_call x1, Pallas kernels, local(): pl.pallas_call(functools.partial(kernel, sizes), out_shape=[pltpu.VMEM(sh...  19.1 us
    pallas_call x1, Pallas kernels, local(): pl.pallas_call(finish, out_shape=[jax.ShapeDtypeStruct(current.shape, f32...  1.34 us

profile of v5, /device:TPU:0, one launch (start us, length us, event | category | flops | bytes accessed | tf_op | source)
XLA Modules:
  0.0 21.1 jit_solution(9622663974233510506)
XLA Ops:
  0.6 19.1 %shard_map.76 = (f32[128,1024]{1,0:T(8,128)S(1)}, f32[144,1024]{1,0:T(8,128)S(1)}, f32[128,1024]{1,0:T(8,128)S(1)}, f32[144,1024]{1,0:T(8,128)S(1)}, f32[128,1024]{1,0:T(8,128)S(1)}, /*index=5*/f32[8,128]{1,0:T(8,128)S(1)}) custom-call(f32[1,128,1024]{2,1,0:T(8,128)} %cur_hbm.1, s32[1,128,1024]{2,1,0:T(8,128)} %cls_hbm.1, f32[1,8]{1,0:T(1,128)} %table.1, ...), custom_call_target="tpu_custom_call" | custom-call | tf_op jit(solution)/shard_map/pallas_call | solution.py:386
  19.7 1.3 %shard_map.77 = (f32[1,128,1024]{2,1,0:T(8,128)}, f32[1,128,1024]{2,1,0:T(8,128)}, f32[1,128,1024]{2,1,0:T(8,128)}) custom-call(f32[128,1024]{1,0:T(8,128)S(1)} %get-tuple-element.9.cur, f32[144,1024]{1,0:T(8,128)S(1)} %get-tuple-element.10.zed, f32[128,1024]{1,0:T(8,128)S(1)} %get-tuple-element.11.wed, f32[144,1024]{1,0:T(8,128)S(1)} %get-tuple-element.12.yed, ...), custom_call_target="tpu_custom_call" | custom-call | tf_op jit(solution)/shard_map/pallas_call | solution.py:403
